TPU v7x, 32 devices: a whole 2x2x4 slice. The times are simulated.
32 devices in a mesh: fsdp: 2 (over x), context: 4 (over z), tensor: 4 (over y, core).
Axes of the slice: x: 2, y: 2, z: 4, core: 2. Of those that a mesh axis runs over, the one named last changes fastest.
Arguments:
- activations: bfloat16 [2, 2048, 1152], P('fsdp', 'context'), may hold values from -6 to 6
- positions: int32 [2, 2048], P('fsdp', 'context'), may hold values from 0 to 2047, as said below
- seg_ids: int32 [2, 2048], P('fsdp', 'context'), may hold values from 0 to 3, as said below
- norm_gains: bfloat16 [4, 1152], P(None, ('fsdp', 'context')), may hold values from 0.5 to 1.5
- head_gains: bfloat16 [2, 256], P(None, ('fsdp', 'context')), may hold values from 0.25 to 1.75
- w_query: bfloat16 [1152, 1024], P(('fsdp', 'context'), 'tensor'), may hold values from -0.1875 to 0.1875
- w_keyval: bfloat16 [1152, 512], P(('fsdp', 'context')), may hold values from -0.1875 to 0.1875
- w_out: bfloat16 [1152, 1024], P(('fsdp', 'context'), 'tensor'), may hold values from -0.1875 to 0.1875
- w_gateup: bfloat16 [1152, 2, 6912], P(('fsdp', 'context'), None, 'tensor'), may hold values from -0.1875 to 0.1875
- w_down: bfloat16 [1152, 6912], P(('fsdp', 'context'), 'tensor'), may hold values from -0.078125 to 0.078125
- cotangent: bfloat16 [2, 2048, 1152], P('fsdp', 'context'), may hold values from -6 to 6
Outputs:
- block_output: bfloat16 [2, 2048, 1152], P('fsdp', 'context')
- input_grad: bfloat16 [2, 2048, 1152], P('fsdp', 'context')
- norm_gains_grad: float32 [4, 1152], P(None, ('fsdp', 'context'))
- head_gains_grad: float32 [2, 256], P(None, ('fsdp', 'context'))
- w_query_grad: float32 [1152, 1024], P(('fsdp', 'context'), 'tensor')
- w_keyval_grad: float32 [1152, 512], P(('fsdp', 'context'))
- w_out_grad: float32 [1152, 1024], P(('fsdp', 'context'), 'tensor')
- w_gateup_grad: float32 [1152, 2, 6912], P(('fsdp', 'context'), None, 'tensor')
- w_down_grad: float32 [1152, 6912], P(('fsdp', 'context'), 'tensor')
Inputs may be any that keep to these rules, and one draw needn't show every extreme that they name: `positions`: within a sequence, a document is a run of consecutive tokens with one document number; numbers never fall along a sequence. Positions are 0 at a document's first token and rise by one from token to token inside it. The first sequence is one document. `seg_ids`: document numbers of a sequence start at 0 and never fall along it.
All inputs are finite; a program needn't handle non-finite values.
Results may differ from a plain program's by a relative error of at most 0.024.
Values may be sent and summed in bfloat16 or wider, within the bound.
A program may use at most 192 MiB of HBM per device.

v0:
```python
import jax
import jax.numpy as jnp
from jax import lax
from jax.sharding import PartitionSpec as P

HD = 256
WINDOW = 512
EPSILON = 1e-06


def from_behind(block, axis, distance):
    devices = range(lax.axis_size(axis))
    route = [(i - distance, i) for i in devices if i - distance in devices]
    return lax.ppermute(block, axis, route)


def rms_norm(values, gain):
    factor = lax.rsqrt(jnp.mean(values * values, axis=-1, keepdims=True) + EPSILON)
    return values * factor * gain


def rotate(tensor, places):
    width_all = tensor.shape[-1]
    half_width = width_all // 2
    freqs = jnp.power(10000.0, -jnp.arange(half_width, dtype=jnp.float32) * 2.0 / width_all)
    angles = places.astype(jnp.float32)[:, None] * freqs[None, :]
    cosine = jnp.cos(angles)[:, None, :]
    sine = jnp.sin(angles)[:, None, :]
    first_half = tensor[..., :half_width]
    second_half = tensor[..., half_width:]
    return jnp.concatenate(
        [first_half * cosine - second_half * sine, second_half * cosine + first_half * sine],
        axis=-1,
    )


def glu(gate_up):
    return jax.nn.gelu(gate_up[:, 0], approximate=True) * gate_up[:, 1]


def contract_last(left_side, right_side):
    return lax.dot_general(
        left_side, right_side, (((1,), (1,)), ((), ())), preferred_element_type=jnp.float32
    )


def contract_first(left_side, right_side):
    return lax.dot_general(
        left_side, right_side, (((0,), (0,)), ((), ())), preferred_element_type=jnp.float32
    )


def shards(
    activations,
    positions,
    seg_ids,
    norm_gains,
    head_gains,
    w_query,
    w_keyval,
    w_out,
    w_gateup,
    w_down,
    cotangent,
):
    tokens = activations.shape[1]
    local_heads = w_query.shape[1] // HD
    inputs = activations[0].astype(jnp.float32)
    places = positions[0]
    documents = seg_ids[0]
    gains_all, heads_all, query_all, keyval_all, out_all = (
        lax.all_gather(norm_gains, ("fsdp", "context"), axis=1, tiled=True),
        lax.all_gather(head_gains, ("fsdp", "context"), axis=1, tiled=True),
        lax.all_gather(w_query, ("fsdp", "context"), axis=0, tiled=True),
        lax.all_gather(w_keyval, ("fsdp", "context"), axis=0, tiled=True),
        lax.all_gather(w_out, ("fsdp", "context"), axis=0, tiled=True),
    )
    gains_f = gains_all.astype(jnp.float32)
    heads_f = heads_all.astype(jnp.float32)
    normed_f, input_back = jax.vjp(rms_norm, inputs, gains_f[0])
    normed = normed_f.astype(jnp.bfloat16)
    query_raw = jnp.dot(normed, query_all, preferred_element_type=jnp.float32).reshape(
        tokens, local_heads, HD
    )
    keyval_raw = jnp.dot(normed, keyval_all, preferred_element_type=jnp.float32)

    def prepare(raw_heads, head_gain):
        return rotate(rms_norm(raw_heads, head_gain), places)

    query_rot, query_back = jax.vjp(prepare, query_raw, heads_f[0])
    key_rot, key_back = jax.vjp(prepare, keyval_raw[:, None, :HD], heads_f[1])
    queries = query_rot.astype(jnp.bfloat16)
    own_keyval = jnp.concatenate([key_rot[:, 0], keyval_raw[:, HD:]], axis=1).astype(jnp.bfloat16)
    labels = jnp.stack([places, documents])
    keep_from = tokens - tokens
    left_keyval, left_labels = from_behind((own_keyval, labels), "context", 1)
    keys_all = jnp.concatenate([left_keyval, own_keyval], axis=0)
    key_places = jnp.concatenate([left_labels[0], places])
    key_documents = jnp.concatenate([left_labels[1], documents])
    has_left = lax.axis_index("context") > 0
    key_live = jnp.concatenate([jnp.full((tokens,), has_left), jnp.ones((tokens,), dtype=bool)])
    scale_factor = HD ** (-0.5)
    block_rows = 512
    block_starts = jnp.arange(tokens // block_rows) * block_rows

    def block_scores():
        spacing = places[:, None] - key_places[None, :]
        visible = (
            key_live[None, :]
            & (documents[:, None] == key_documents[None, :])
            & (spacing >= 0)
            & (spacing < WINDOW)
        )
        raw_scores = (
            jnp.einsum("qhd,kd->hqk", queries, keys_all[:, :HD], preferred_element_type=jnp.float32)
            * scale_factor
        )
        return (jnp.where(visible[None], raw_scores, -1e30), keys_all, queries)

    def forward_block(start):
        scores, near_keyval, query_block = block_scores()
        row_top = jnp.max(scores, axis=-1, keepdims=True)
        raised = jnp.exp(scores - row_top)
        row_total = jnp.sum(raised, axis=-1, keepdims=True)
        probs = raised / row_total
        mixed_block = jnp.einsum(
            "hqk,kd->qhd",
            probs.astype(jnp.bfloat16),
            near_keyval[:, HD:],
            preferred_element_type=jnp.float32,
        )
        return (mixed_block.astype(jnp.bfloat16), row_top + jnp.log(row_total))

    mixed_blocks, log_blocks = lax.map(forward_block, block_starts)
    mixed_low = mixed_blocks.reshape(tokens, local_heads * HD)
    branch = lax.psum(contract_last(mixed_low, out_all).astype(jnp.bfloat16), "tensor").astype(
        jnp.float32
    )
    post_attn, post_attn_back = jax.vjp(rms_norm, branch, gains_f[1])
    hidden = inputs + post_attn
    normed_mlp_f, pre_mlp_back = jax.vjp(rms_norm, hidden, gains_f[2])
    normed_mlp = normed_mlp_f.astype(jnp.bfloat16)
    columns = normed_mlp
    gate_up = jnp.einsum(
        "bn,nkf->bkf",
        columns,
        lax.all_gather(w_gateup, ("fsdp", "context"), axis=0, tiled=True),
        preferred_element_type=jnp.float32,
    )
    active_f, glu_back = jax.vjp(glu, gate_up)
    active = active_f.astype(jnp.bfloat16)
    down = lax.psum(
        contract_last(
            active, lax.all_gather(w_down, ("fsdp", "context"), axis=0, tiled=True)
        ).astype(jnp.bfloat16),
        "tensor",
    ).astype(jnp.float32)
    post_mlp, post_mlp_back = jax.vjp(rms_norm, down, gains_f[3])
    result = hidden + post_mlp
    grad_out = cotangent[0].astype(jnp.float32)
    d_down, gain_post_mlp = post_mlp_back(grad_out)
    down_low = d_down.astype(jnp.bfloat16)
    columns = down_low
    d_active = jnp.dot(
        columns,
        lax.all_gather(w_down, ("fsdp", "context"), axis=0, tiled=True),
        preferred_element_type=jnp.float32,
    )
    d_gate_up = glu_back(d_active)[0].astype(jnp.bfloat16)
    d_normed_part = jnp.einsum(
        "bkf,nkf->bn",
        d_gate_up,
        lax.all_gather(w_gateup, ("fsdp", "context"), axis=0, tiled=True),
        preferred_element_type=jnp.float32,
    )
    d_normed_mlp = lax.psum(d_normed_part.astype(jnp.bfloat16), "tensor").astype(jnp.float32)
    d_hidden_norm, gain_pre_mlp = pre_mlp_back(d_normed_mlp)
    d_hidden = grad_out + d_hidden_norm
    features = normed_mlp
    grad_cols = down_low
    gate_up_term = jnp.einsum(
        "bn,bkf->nkf", features, d_gate_up, preferred_element_type=jnp.float32
    )
    down_term = contract_first(grad_cols, active)
    scatter = lambda part: lax.psum_scatter(
        part.astype(jnp.bfloat16), ("fsdp", "context"), scatter_dimension=0, tiled=True
    ).astype(jnp.float32)
    gate_grad = scatter(gate_up_term[:, 0])
    up_grad = scatter(gate_up_term[:, 1])
    down_grad = scatter(down_term)
    d_branch, gain_post_attn = post_attn_back(d_hidden)
    branch_low = d_branch.astype(jnp.bfloat16)
    d_mixed = jnp.dot(branch_low, out_all, preferred_element_type=jnp.float32)
    d_mixed_low = d_mixed.astype(jnp.bfloat16).reshape(tokens, local_heads, HD)

    def backward_block(carry, item):
        start, log_block = item
        scores, near_keyval, query_block = block_scores()
        probs_again = jnp.exp(scores - log_block)
        d_probs = jnp.einsum(
            "qhd,kd->hqk", d_mixed_low, near_keyval[:, HD:], preferred_element_type=jnp.float32
        )
        row_inner = jnp.sum(probs_again * d_probs, axis=-1, keepdims=True)
        d_scores = (probs_again * (d_probs - row_inner)).astype(jnp.bfloat16)
        d_query_block = (
            jnp.einsum(
                "hqk,kd->qhd", d_scores, near_keyval[:, :HD], preferred_element_type=jnp.float32
            )
            * scale_factor
        )
        d_keys = (
            jnp.einsum("hqk,qhd->kd", d_scores, query_block, preferred_element_type=jnp.float32)
            * scale_factor
        )
        d_values = jnp.einsum(
            "hqk,qhd->kd",
            probs_again.astype(jnp.bfloat16),
            d_mixed_low,
            preferred_element_type=jnp.float32,
        )
        updated = carry + jnp.concatenate([d_keys, d_values], axis=1)
        return (updated, d_query_block)

    d_keyval, d_query_blocks = lax.scan(
        backward_block,
        jnp.zeros((tokens + tokens, 2 * HD), jnp.float32),
        (block_starts, log_blocks),
    )
    d_queries = d_query_blocks.reshape(tokens, local_heads, HD)
    returned = from_behind(d_keyval[:tokens].astype(jnp.bfloat16), "context", -1).astype(
        jnp.float32
    )
    own_grad = d_keyval[tokens:].at[keep_from:].add(returned)
    d_query_raw, gain_query = query_back(d_queries)
    d_query_low = d_query_raw.reshape(tokens, local_heads * HD).astype(jnp.bfloat16)
    d_normed_query, keyval_grad, gain_query_all = (
        lax.psum(contract_last(d_query_low, query_all).astype(jnp.bfloat16), "tensor").astype(
            jnp.float32
        ),
        lax.psum(own_grad.astype(jnp.bfloat16), "tensor").astype(jnp.float32),
        lax.psum(gain_query.astype(jnp.bfloat16), "tensor").astype(jnp.float32),
    )
    d_key_raw, gain_key = key_back(keyval_grad[:, None, :HD])
    d_keyval_low = jnp.concatenate([d_key_raw[:, 0], keyval_grad[:, HD:]], axis=1).astype(
        jnp.bfloat16
    )
    d_normed = d_normed_query + contract_last(d_keyval_low, keyval_all)
    d_input_norm, gain_input = input_back(d_normed)
    input_total = d_hidden + d_input_norm
    features = normed
    grad_cols = branch_low
    attn_grads = lax.psum_scatter(
        jnp.stack(
            [contract_first(features, d_query_low), contract_first(grad_cols, mixed_low)], axis=1
        ).astype(jnp.bfloat16),
        ("fsdp", "context"),
        scatter_dimension=0,
        tiled=True,
    ).astype(jnp.float32)
    keyval_term = contract_first(normed, d_keyval_low)
    gain_terms = jnp.stack([gain_input, gain_post_attn, gain_pre_mlp, gain_post_mlp])
    head_terms = jnp.stack([gain_query_all, gain_key])
    gain_grad, head_grad, keyval_weight_grad = (
        lax.psum_scatter(
            gain_terms.astype(jnp.bfloat16), ("fsdp", "context"), scatter_dimension=1, tiled=True
        ).astype(jnp.float32),
        lax.psum_scatter(
            head_terms.astype(jnp.bfloat16), ("fsdp", "context"), scatter_dimension=1, tiled=True
        ).astype(jnp.float32),
        lax.psum_scatter(
            keyval_term.astype(jnp.bfloat16), ("fsdp", "context"), scatter_dimension=0, tiled=True
        ).astype(jnp.float32),
    )
    return (
        result[None].astype(jnp.bfloat16),
        input_total[None].astype(jnp.bfloat16),
        gain_grad,
        head_grad,
        attn_grads[:, 0],
        keyval_weight_grad,
        attn_grads[:, 1],
        jnp.stack([gate_grad, up_grad], axis=1),
        down_grad,
    )


def solution(mesh):
    return jax.shard_map(
        shards,
        mesh=mesh,
        in_specs=(
            P("fsdp", "context", None),
            P("fsdp", "context"),
            P("fsdp", "context"),
            P(None, ("fsdp", "context")),
            P(None, ("fsdp", "context")),
            P(("fsdp", "context"), "tensor"),
            P(("fsdp", "context"), None),
            P(("fsdp", "context"), "tensor"),
            P(("fsdp", "context"), None, "tensor"),
            P(("fsdp", "context"), "tensor"),
            P("fsdp", "context", None),
        ),
        out_specs=(
            P("fsdp", "context", None),
            P("fsdp", "context", None),
            P(None, ("fsdp", "context")),
            P(None, ("fsdp", "context")),
            P(("fsdp", "context"), "tensor"),
            P(("fsdp", "context"), None),
            P(("fsdp", "context"), "tensor"),
            P(("fsdp", "context"), None, "tensor"),
            P(("fsdp", "context"), "tensor"),
        ),
        check_vma=False,
    )
```

profile of v0, /device:TPU:0, one launch (start us, length us, event | category | flops | bytes accessed | tf_op | source)
XLA Modules:
  0.0 1111.7 jit_solution(1959116816128827641)
XLA Ops:
  8.7 4.9 collective-permute-start.1
  14.3 18.8 %all-gather.1 = bf16[8,32,2]{1,2,0:T(2,128)(2,1)S(1)} all-gather(bf16[1,32,2]{1,2,0:T(2,128)(2,1)} %bitcast.266), channel_id=1, replica_groups=mesh['fsdp'=2,'context'=4,'tensor'=4] {'fsdp','context'}, dimensions={0}, use_global_device_ids=true | all-gather | bytes 1152 | tf_op jit(solution)/shard_map/all_gather | solution.py:73
  33.2 27.2 %all-gather = bf16[8,144,4]{1,2,0:T(4,128)(2,1)S(1)} all-gather(bf16[1,144,4]{1,2,0:T(4,128)(2,1)} %bitcast.265), channel_id=1, replica_groups=mesh['fsdp'=2,'context'=4,'tensor'=4] {'fsdp','context'}, dimensions={0}, use_global_device_ids=true | all-gather | bytes 10368 | tf_op jit(solution)/shard_map/all_gather | solution.py:72
  61.1 1.6 fusion.30
  62.8 32.5 %all_gather.26 = bf16[1152,256]{1,0:T(8,128)(2,1)S(1)} all-gather(bf16[144,256]{1,0:T(8,128)(2,1)} %param.20), channel_id=1, replica_groups=mesh['fsdp'=2,'context'=4,'tensor'=4] {'fsdp','context'}, dimensions={0}, use_global_device_ids=true | all-gather | bytes 663552 | tf_op jit(solution)/shard_map/all_gather | solution.py:74
  96.1 2.0 multiply_reduce_fusion.1
  99.1 2.2 fusion.131
  103.0 1.3 collective-permute-start
  104.4 33.8 %all_gather.27 = bf16[1152,256]{1,0:T(8,128)(2,1)S(1)} all-gather(bf16[144,256]{1,0:T(8,128)(2,1)S(1)} %copy-done.32), channel_id=1, replica_groups=mesh['fsdp'=2,'context'=4,'tensor'=4] {'fsdp','context'}, dimensions={0}, use_global_device_ids=true | all-gather | bytes 663552 | tf_op jit(solution)/shard_map/all_gather | solution.py:76
  138.4 2.0 fusion.140
  141.4 1.6 convolution_convert_fusion.5
  143.1 2.3 copy.32
  146.2 36.1 %all-reduce.13.cloned.1.call-done = bf16[512,1152]{1,0:T(8,128)(2,1)} async-done(((bf16[512,1152]{1,0:T(8,128)(2,1)}), bf16[512,1152]{1,0:T(8,128)(2,1)}) %all-reduce.13.cloned.1.call-update) | async-done | bytes 1179664 | tf_op jit(solution)/shard_map/psum | solution.py:136
  182.3 1.7 fusion.39
  185.1 2.3 multiply_reduce_fusion
  188.6 119.4 %all-gather.8.cloned.1.call-done = bf16[1152,2,1728]{2,0,1:T(8,128)(2,1)} async-done(((bf16[144,2,1728]{2,0,1:T(8,128)(2,1)}), bf16[1152,2,1728]{2,0,1:T(8,128)(2,1)}) %all-gather.8.cloned.1.call-update) | async-done | bytes 7962640 | tf_op jit(solution)/shard_map/all_gather | solution.py:147
  308.0 8.2 fusion.114
  316.2 2.9 copy-done.8
  319.1 2.4 multiply_convert_fusion
  321.5 58.5 %all-gather.10.cloned.1.call-done = bf16[1152,1728]{1,0:T(8,128)(2,1)} async-done(((bf16[144,1728]{1,0:T(8,128)(2,1)}), bf16[1152,1728]{1,0:T(8,128)(2,1)}) %all-gather.10.cloned.1.call-update) | async-done | bytes 3981328 | tf_op jit(solution)/shard_map/all_gather | solution.py:154
  380.0 6.3 convolution_convert_fusion.4
  386.6 36.0 %all-reduce.15.cloned.1.call-done = bf16[512,1152]{1,0:T(8,128)(2,1)} async-done(((bf16[512,1152]{1,0:T(8,128)(2,1)}), bf16[512,1152]{1,0:T(8,128)(2,1)}) %all-reduce.15.cloned.1.call-update) | async-done | bytes 1179664 | tf_op jit(solution)/shard_map/psum | solution.py:152
  422.7 1.7 fusion.41
  424.4 3.4 fusion.38
  427.9 10.7 multiply_bitcast_fusion
  438.6 1.7 copy-done.82
  440.3 8.1 fusion.7
  448.9 1.3 log_add_fusion
  450.2 36.1 %all-reduce.17.cloned.1.call-done = bf16[512,1152]{1,0:T(8,128)(2,1)} async-done(((bf16[512,1152]{1,0:T(8,128)(2,1)}), bf16[512,1152]{1,0:T(8,128)(2,1)}) %all-reduce.17.cloned.1.call-update) | async-done | bytes 1179664 | tf_op jit(solution)/shard_map/psum | solution.py:176
  486.4 3.6 fusion.29
  490.1 5.1 fusion.25
  501.8 1.4 collective-permute-start.2
  504.2 1.6 convolution_convert_fusion.3
  505.7 11.6 %collective-permute-done.2 = bf16[512,512]{0,1:T(8,128)(2,1)S(1)} collective-permute-done((bf16[512,512]{0,1:T(8,128)(2,1)S(1)}, bf16[512,512]{0,1:T(8,128)(2,1)S(1)}, u32[]{:S(2)}, u32[]{:S(2)}) %collective-permute-start.2) | collective-permute-done | bytes 524320 | tf_op jit(solution)/shard_map/ppermute | solution.py:14
  518.4 1.4 reshape.553
  519.7 1.3 reshape.552
  523.5 7.2 psum.47
  530.7 2.3 fusion.22
  533.0 2.5 fusion.21
  535.6 27.2 %all-reduce.19.cloned.1.call-done = (bf16[512,1152]{1,0:T(8,128)(2,1)}, bf16[512,512]{0,1:T(8,128)(2,1)}) async-done(((bf16[512,1152]{1,0:T(8,128)(2,1)}, bf16[512,512]{0,1:T(8,128)(2,1)}), (bf16[512,1152]{1,0:T(8,128)(2,1)}, bf16[512,512]{0,1:T(8,128)(2,1)})) %all-reduce.19.cloned.1.call-update) | async-done | bytes 1703952 | tf_op jit(solution)/shard_map/psum | solution.py:237
  565.7 3.2 fusion.27
  570.1 1.4 copy.36
  571.6 1.4 pad_maximum_fusion.9
  573.0 1.6 copy.34
  576.1 3.1 convolution_convert_fusion.2
  579.3 9.3 convolution_convert_fusion
  588.6 3.5 slice_bitcast_fusion.1
  592.1 6.5 copy.38
  598.6 6.5 copy.40
  606.8 6.3 convolution_convert_fusion.1
  613.8 4.0 fusion.52
  617.8 16.4 %reduce-scatter.24.cloned.1.call-done = bf16[32,2]{1,0:T(8,128)(2,1)} async-done(((bf16[256,2]{1,0:T(8,128)(2,1)}), bf16[32,2]{1,0:T(8,128)(2,1)}) %reduce-scatter.24.cloned.1.call-update) | async-done | bytes 144
  635.6 60.7 %reduce-scatter.22.cloned.1.call-done = bf16[144,4]{1,0:T(8,128)(2,1)} async-done(((bf16[1152,4]{1,0:T(8,128)(2,1)}), bf16[144,4]{1,0:T(8,128)(2,1)}) %reduce-scatter.22.cloned.1.call-update) | async-done | bytes 1168
  697.8 65.6 %reduce-scatter.16.cloned.1.call-done = bf16[144,2,256]{2,0,1:T(8,128)(2,1)} async-done(((bf16[1152,2,256]{2,0,1:T(8,128)(2,1)}), bf16[144,2,256]{2,0,1:T(8,128)(2,1)}) %reduce-scatter.16.cloned.1.call-update) | async-done | bytes 147472 | tf_op jit(solution)/shard_map/reduce_scatter | solution.py:252
  765.0 65.4 %reduce-scatter.18.cloned.1.call-done = bf16[144,512]{1,0:T(8,128)(2,1)} async-done(((bf16[1152,512]{1,0:T(8,128)(2,1)}), bf16[144,512]{1,0:T(8,128)(2,1)}) %reduce-scatter.18.cloned.1.call-update) | async-done | bytes 147472 | tf_op jit(solution)/shard_map/reduce_scatter | solution.py:270
  830.4 1.7 convert_element_type.217
  832.1 88.7 %reduce-scatter.26.cloned.1.call-done = bf16[144,1728]{1,0:T(8,128)(2,1)} async-done(((bf16[1152,1728]{1,0:T(8,128)(2,1)}), bf16[144,1728]{1,0:T(8,128)(2,1)}) %reduce-scatter.26.cloned.1.call-update) | async-done | bytes 497680
  920.8 2.3 copy.39
  923.1 88.9 %reduce-scatter.28.cloned.1.call-done = bf16[144,1728]{1,0:T(8,128)(2,1)} async-done(((bf16[1152,1728]{1,0:T(8,128)(2,1)}), bf16[144,1728]{1,0:T(8,128)(2,1)}) %reduce-scatter.28.cloned.1.call-update) | async-done | bytes 497680
  1011.9 2.3 copy.41
  1014.2 1.9 maximum_convert_fusion
  1016.1 3.2 copy.33
  1019.2 83.7 %reduce-scatter.20.cloned.1.call-done = bf16[144,1728]{1,0:T(8,128)(2,1)} async-done(((bf16[1152,1728]{1,0:T(8,128)(2,1)}), bf16[144,1728]{1,0:T(8,128)(2,1)}) %reduce-scatter.20.cloned.1.call-update) | async-done | bytes 497680 | tf_op jit(solution)/shard_map/reduce_scatter | solution.py:185
  1102.9 2.1 convert_element_type.221
  (263 shorter events, 34.7 us)
Async XLA Ops:
  7.2 91.9 %all-gather.6.cloned.1.call-start = ((), (), s32[]{:S(2)}) async-start(), calls=%async_computation.7 | async-start | bytes 1327104 | tf_op jit(solution)/shard_map/all_gather | solution.py:75
  7.9 174.4 %all-reduce.13.cloned.1.call-start = ((), (), s32[]{:S(2)}) async-start(), calls=%async_computation.8 | async-start | bytes 2359296 | tf_op jit(solution)/shard_map/psum | solution.py:136
  8.7 129.6 %collective-permute-start.1 = (s32[2,512]{1,0:T(2,128)S(1)}, s32[2,512]{1,0:T(2,128)S(1)}, u32[]{:S(2)}, u32[]{:S(2)}) collective-permute-start(s32[2,512]{1,0:T(2,128)S(1)} %pad_add_fusion.2), channel_id=1, source_target_pairs={{0,4},{4,8},{8,12},{1,5},{5,9},{9,13},{2,6},{6,10},{10,14},{3,7},{... | collective-permute-start | bytes 12296 | tf_op jit(solution)/shard_map/ppermute | solution.py:14
  14.3 87.4 %copy-start.37 = (f32[512]{0:T(512)}, f32[512]{0:T(512)S(1)}, u32[]{:S(2)}) copy-start(f32[512]{0:T(512)S(1)} %convert_element_type.178) | copy-start | bytes 6148
  60.5 41.2 %copy-start.73 = (f32[128]{0:T(128)}, f32[128]{0:T(128)S(1)}, u32[]{:S(2)}) copy-start(f32[128]{0:T(128)S(1)} %multiply_power_fusion) | copy-start | bytes 1540
  61.1 38.0 %copy-start.44 = (f32[1152]{0:T(1024)}, f32[1152]{0:T(1024)S(1)}, u32[]{:S(2)}) copy-start(f32[1152]{0:T(1024)S(1)} %get-tuple-element.146) | copy-start | bytes 13828
  62.7 36.3 %copy-start.52 = (f32[512]{0:T(512)}, f32[512]{0:T(512)S(1)}, u32[]{:S(2)}) copy-start(f32[512]{0:T(512)S(1)} %fusion.30) | copy-start | bytes 6148
  62.7 36.4 %copy-start.70 = (f32[512]{0:T(512)}, f32[512]{0:T(512)S(1)}, u32[]{:S(2)}) copy-start(f32[512]{0:T(512)S(1)} %fusion.116) | copy-start | bytes 6148
  62.7 36.3 %copy-start.63 = (f32[1,256]{1,0:T(1,128)}, f32[1,256]{1,0:T(1,128)S(1)}, u32[]{:S(2)}) copy-start(f32[1,256]{1,0:T(1,128)S(1)} %get-tuple-element.171) | copy-start | bytes 3076
  62.8 38.8 %copy-start.61 = (f32[1,256]{1,0:T(1,128)}, f32[1,256]{1,0:T(1,128)S(1)}, u32[]{:S(2)}) copy-start(f32[1,256]{1,0:T(1,128)S(1)} %get-tuple-element.172) | copy-start | bytes 3076
  62.8 36.3 %copy-start.1 = (bf16[1,512,1152]{2,1,0:T(8,128)(2,1)S(1)}, bf16[1,512,1152]{2,1,0:T(8,128)(2,1)}, u32[]{:S(2)}) copy-start(bf16[1,512,1152]{2,1,0:T(8,128)(2,1)} %param.15) | copy-start | bytes 3538948
  98.1 3.2 copy-start.42
  101.5 36.7 %copy-start.60 = (s32[1,512]{1,0:T(1,128)S(1)}, s32[1,512]{1,0:T(1,128)}, u32[]{:S(2)}) copy-start(s32[1,512]{1,0:T(1,128)} %param.16) | copy-start | bytes 6148
  101.6 36.7 %copy-start.67 = (s32[1,512]{1,0:T(1,128)S(1)}, s32[1,512]{1,0:T(1,128)}, u32[]{:S(2)}) copy-start(s32[1,512]{1,0:T(1,128)} %param.17) | copy-start | bytes 6148
  103.0 35.3 %collective-permute-start = (bf16[512,512]{0,1:T(8,128)(2,1)S(1)}, bf16[512,512]{0,1:T(8,128)(2,1)S(1)}, u32[]{:S(2)}, u32[]{:S(2)}) collective-permute-start(bf16[512,512]{0,1:T(8,128)(2,1)S(1)} %pad_maximum_fusion.2), channel_id=1, source_target_pairs={{0,4},{4,8},{8,12},{1,5},{5,9},{9,13},{2,6},{6,10},{10,14},{3,7},{... | collective-permute-start | bytes 1572872 | tf_op jit(solution)/shard_map/ppermute | solution.py:14
  138.2 3.1 copy-start.20
  141.4 3.9 copy-start.26
  143.0 165.0 %all-gather.8.cloned.1.call-start = ((), (), s32[]{:S(2)}) async-start(), calls=%async_computation.9 | async-start | bytes 9289728 | tf_op jit(solution)/shard_map/all_gather | solution.py:147
  145.4 234.7 %all-gather.10.cloned.1.call-start = ((), (), s32[]{:S(2)}) async-start(), calls=%async_computation.10 | async-start | bytes 4644864 | tf_op jit(solution)/shard_map/all_gather | solution.py:154
  145.9 276.7 %all-reduce.15.cloned.1.call-start = ((), (), s32[]{:S(2)}) async-start(), calls=%async_computation.11 | async-start | bytes 2359296 | tf_op jit(solution)/shard_map/psum | solution.py:152
  182.3 125.7 %copy-start = (bf16[512,1152]{1,0:T(8,128)(2,1)S(1)}, bf16[512,1152]{1,0:T(8,128)(2,1)}, u32[]{:S(2)}) copy-start(bf16[512,1152]{1,0:T(8,128)(2,1)} %all-reduce.13.cloned.1.call-done) | copy-start | bytes 3538948
  386.4 100.0 %all-reduce.17.cloned.1.call-start = ((), (), s32[]{:S(2)}) async-start(), calls=%async_computation.12 | async-start | bytes 2359296 | tf_op jit(solution)/shard_map/psum | solution.py:176
  422.7 5.2 copy-start.5
  422.7 5.2 copy-start.12
  424.4 14.2 %copy-start.47 = (f32[512]{0:T(512)}, f32[512]{0:T(512)S(1)}, u32[]{:S(2)}) copy-start(f32[512]{0:T(512)S(1)} %fusion.121) | copy-start | bytes 6148
  424.4 15.9 %slice-start = ((s8[8257536]{0:T(1024)(128)(4,1)}), s8[4194304]{0:T(1024)(128)(4,1)S(1)}, s32[]{:S(2)}) async-start(s8[8257536]{0:T(1024)(128)(4,1)} %bitcast.267), calls=%async_computation.21 | async-start | bytes 8388608
  427.8 10.7 copy-start.77
  427.9 12.5 %slice-start.1 = ((s8[8257536]{0:T(1024)(128)(4,1)}), s8[4063232]{0:T(1024)(128)(4,1)S(1)}, s32[]{:S(2)}) async-start(s8[8257536]{0:T(1024)(128)(4,1)} %bitcast.267), calls=%async_computation.22 | async-start | bytes 8126464
  448.5 114.3 %all-reduce.19.cloned.1.call-start = ((), (), s32[]{:S(2)}) async-start(), calls=%async_computation.20 | async-start | bytes 3407872 | tf_op jit(solution)/shard_map/psum | solution.py:237
  486.4 3.7 copy-start.59
  486.4 3.7 copy-start.2
  486.4 3.7 copy-start.6
  486.4 3.7 copy-start.11
  486.4 3.7 copy-start.30
  486.4 3.7 copy-start.34
  486.4 3.7 copy-start.48
  486.4 3.7 copy-start.50
  490.1 5.1 copy-start.57
  500.5 3.4 copy-start.66
  501.8 15.5 %collective-permute-start.2 = (bf16[512,512]{0,1:T(8,128)(2,1)S(1)}, bf16[512,512]{0,1:T(8,128)(2,1)S(1)}, u32[]{:S(2)}, u32[]{:S(2)}) collective-permute-start(bf16[512,512]{0,1:T(8,128)(2,1)S(1)} %fusion.66), channel_id=1, source_target_pairs={{4,0},{8,4},{12,8},{5,1},{9,5},{13,9},{6,2},{10,6},{14,10},{7,3},{... | collective-permute-start | bytes 1572872 | tf_op jit(solution)/shard_map/ppermute | solution.py:14
  504.1 13.2 %copy-start.25 = (bf16[512,256]{0,1:T(8,128)(2,1)}, bf16[512,256]{0,1:T(8,128)(2,1)S(1)}, u32[]{:S(2)}) copy-start(bf16[512,256]{0,1:T(8,128)(2,1)S(1)} %fusion.108) | copy-start | bytes 786436
  505.7 25.0 %copy-start.17 = (bf16[512,1152]{1,0:T(8,128)(2,1)S(1)}, bf16[512,1152]{1,0:T(8,128)(2,1)}, u32[]{:S(2)}) copy-start(bf16[512,1152]{1,0:T(8,128)(2,1)} %copy-done.16) | copy-start | bytes 3538948
  518.3 14.7 %copy-start.3 = (bf16[1,512,1152]{2,1,0:T(8,128)(2,1)S(1)}, bf16[1,512,1152]{2,1,0:T(8,128)(2,1)}, u32[]{:S(2)}) copy-start(bf16[1,512,1152]{2,1,0:T(8,128)(2,1)} %param.15) | copy-start | bytes 3538948
  518.3 115.9 %reduce-scatter.24.cloned.1.call-start = ((), (), s32[]{:S(2)}) async-start(), calls=%async_computation.17 | async-start | bytes 73728
  533.0 31.0 %copy-start.39 = (f32[512]{0:T(512)S(1)}, f32[512]{0:T(512)}, u32[]{:S(2)}) copy-start(f32[512]{0:T(512)} %copy-done.37) | copy-start | bytes 6148
  533.0 31.0 %copy-start.75 = (f32[128]{0:T(128)S(1)}, f32[128]{0:T(128)}, u32[]{:S(2)}) copy-start(f32[128]{0:T(128)} %copy-done.73) | copy-start | bytes 1540
  533.0 32.2 %copy-start.10 = (f32[512,512]{0,1:T(8,128)S(1)}, f32[512,512]{0,1:T(8,128)}, u32[]{:S(2)}) copy-start(f32[512,512]{0,1:T(8,128)} %copy-done.9) | copy-start | bytes 3145732
  533.0 32.2 %copy-start.41 = (f32[512]{0:T(512)S(1)}, f32[512]{0:T(512)}, u32[]{:S(2)}) copy-start(f32[512]{0:T(512)} %copy-done.40) | copy-start | bytes 6148
  533.0 32.2 %copy-start.62 = (f32[1,256]{1,0:T(1,128)S(1)}, f32[1,256]{1,0:T(1,128)}, u32[]{:S(2)}) copy-start(f32[1,256]{1,0:T(1,128)} %copy-done.61) | copy-start | bytes 3076
  535.6 29.9 %copy-start.55 = (f32[512]{0:T(512)S(1)}, f32[512]{0:T(512)}, u32[]{:S(2)}) copy-start(f32[512]{0:T(512)} %copy-done.54) | copy-start | bytes 6148
  564.0 4.9 copy-start.28
  565.6 3.3 copy-start.29
  565.7 3.9 copy-start.76
  565.7 9.0 copy-start.22
  565.7 9.0 copy-start.27
  571.6 124.7 %reduce-scatter.22.cloned.1.call-start = ((), (), s32[]{:S(2)}) async-start(), calls=%async_computation.16 | async-start | bytes 331776
  574.6 188.8 %reduce-scatter.16.cloned.1.call-start = ((), (), s32[]{:S(2)}) async-start(), calls=%async_computation.13 | async-start | bytes 1327104 | tf_op jit(solution)/shard_map/reduce_scatter | solution.py:252
  575.9 3.4 copy-start.31
  575.9 3.4 copy-start.35
  575.9 3.4 copy-start.51
  575.9 254.5 %reduce-scatter.18.cloned.1.call-start = ((), (), s32[]{:S(2)}) async-start(), calls=%async_computation.14 | async-start | bytes 1327104 | tf_op jit(solution)/shard_map/reduce_scatter | solution.py:270
  579.2 341.6 %reduce-scatter.26.cloned.1.call-start = ((), (), s32[]{:S(2)}) async-start(), calls=%async_computation.18 | async-start | bytes 4644864
  598.6 413.3 %reduce-scatter.28.cloned.1.call-start = ((), (), s32[]{:S(2)}) async-start(), calls=%async_computation.19 | async-start | bytes 4644864
  605.2 497.7 %reduce-scatter.20.cloned.1.call-start = ((), (), s32[]{:S(2)}) async-start(), calls=%async_computation.15 | async-start | bytes 4644864 | tf_op jit(solution)/shard_map/reduce_scatter | solution.py:185
  (38 other events, 61.7 us)
Sparse Core Ops, SparseCore 0:
  10.1 43.7 all-gather.5
  143.1 39.0 all-reduce.12
  185.0 122.9 all-gather.7
  310.0 70.0 all-gather.9
  386.5 36.1 all-reduce.14
  448.6 37.7 all-reduce.16
  518.4 44.2 all-reduce.18
  571.7 62.4 reduce-scatter.23
  638.1 58.1 reduce-scatter.21
  699.5 63.8 reduce-scatter.15
  766.8 63.5 reduce-scatter.17
  833.8 86.9 reduce-scatter.25
  924.4 87.5 reduce-scatter.27
  1015.3 87.5 reduce-scatter.19
where the time goes:
time: 1120 us; the launch traced here: 1110 us
  waiting for transfers between devices  796 us (71%)
  blocking collectives  120 us (11%)
  matrix products  72.4 us (6%)
  local copies, waits for them, and re-layouts  50.5 us (5%)
  other arithmetic  49.1 us (4%)
  between operations  15.3 us (1%)
    unnamed x18, waiting for transfers between devices  256 us
    all_gather x1, waiting for transfers between devices, shards(): lax.all_gather(w_gateup, ('fsdp', 'context'), axis=0, tiled=True)  119 us
    reduce_scatter x1, waiting for transfers between devices, shards(): lax.psum_scatter(part.astype(jnp.bfloat16), ('fsdp', 'context'), scatter_...  83.7 us
    reduce_scatter x1, waiting for transfers between devices, shards(): lax.psum_scatter(jnp.stack([contract_first(features, d_query_low), contra...  65.6 us
    reduce_scatter x1, waiting for transfers between devices, shards(): lax.psum_scatter(keyval_term.astype(jnp.bfloat16), ('fsdp', 'context'), s...  65.4 us
    all_gather x1, waiting for transfers between devices, shards(): lax.all_gather(w_down, ('fsdp', 'context'), axis=0, tiled=True)  58.5 us
    unnamed x180, local copies, waits for them, and re-layouts  39.6 us
    psum x1, waiting for transfers between devices, shards(): lax.psum(d_normed_part.astype(jnp.bfloat16), 'tensor').astype(jnp.float32)  36.1 us
  transfers between devices with their start and end apart: 17, of which 14 were waited for; matrix products, arithmetic and copies ran while one was open for 9% of the time, Pallas kernels for 0%

commit v1 on v0

--- a/solution.py
+++ b/solution.py
@@ -63,6 +63,11 @@
     w_down,
     cotangent,
 ):
+
+    def refer_core(m):
+        b_next = lax.all_gather(m, axis_name="tensor")
+        return jnp.sum(b_next, 0)
+
     tokens = activations.shape[1]
     local_heads = w_query.shape[1] // HD
     inputs = activations[0].astype(jnp.float32)
@@ -133,9 +138,7 @@
 
     mixed_blocks, log_blocks = lax.map(forward_block, block_starts)
     mixed_low = mixed_blocks.reshape(tokens, local_heads * HD)
-    branch = lax.psum(contract_last(mixed_low, out_all).astype(jnp.bfloat16), "tensor").astype(
-        jnp.float32
-    )
+    branch = refer_core(contract_last(mixed_low, out_all).astype(jnp.bfloat16)).astype(jnp.float32)
     post_attn, post_attn_back = jax.vjp(rms_norm, branch, gains_f[1])
     hidden = inputs + post_attn
     normed_mlp_f, pre_mlp_back = jax.vjp(rms_norm, hidden, gains_f[2])

time: 1120 us -> 1120 us (level)
    psum x1 -> x0, waiting for transfers between devices: 36.1 us -> none  [shards(): lax.psum(contract_last(mixed_low, out_all).astype(jnp.bfloat16), 'tensor')]
    all_gather x0 -> x1, waiting for transfers between devices: none -> 35.9 us  [refer_core(): b_next = lax.all_gather(m, axis_name='tensor')]
    unnamed x180 -> x178, local copies, waits for them, and re-layouts: 39.6 us -> 39.6 us
where the time goes in v1:
time: 1120 us; the launch traced here: 1110 us
  waiting for transfers between devices  793 us (71%)
  blocking collectives  120 us (11%)
  matrix products  72.5 us (6%)
  other arithmetic  51.1 us (5%)
  local copies, waits for them, and re-layouts  50.4 us (4%)
  between operations  15.3 us (1%)
    unnamed x18, waiting for transfers between devices  256 us
    all_gather x1, waiting for transfers between devices, shards(): lax.all_gather(w_gateup, ('fsdp', 'context'), axis=0, tiled=True)  117 us
    reduce_scatter x1, waiting for transfers between devices, shards(): lax.psum_scatter(part.astype(jnp.bfloat16), ('fsdp', 'context'), scatter_...  83.7 us
    reduce_scatter x1, waiting for transfers between devices, shards(): lax.psum_scatter(jnp.stack([contract_first(features, d_query_low), contra...  65.4 us
    reduce_scatter x1, waiting for transfers between devices, shards(): lax.psum_scatter(keyval_term.astype(jnp.bfloat16), ('fsdp', 'context'), s...  65.4 us
    all_gather x1, waiting for transfers between devices, shards(): lax.all_gather(w_down, ('fsdp', 'context'), axis=0, tiled=True)  58.5 us
    unnamed x178, local copies, waits for them, and re-layouts  39.6 us
    psum x1, waiting for transfers between devices, shards(): lax.psum(d_normed_part.astype(jnp.bfloat16), 'tensor').astype(jnp.float32)  36.1 us
  transfers between devices with their start and end apart: 17, of which 14 were waited for; matrix products, arithmetic and copies ran while one was open for 9% of the time, Pallas kernels for 0%

profile of v1, /device:TPU:0, one launch (start us, length us, event | category | flops | bytes accessed | tf_op | source)
XLA Modules:
  0.0 1111.3 jit_solution(3614129570835466476)
XLA Ops:
  8.7 4.9 collective-permute-start.1
  14.3 18.8 %all-gather.2 = bf16[8,32,2]{1,2,0:T(2,128)(2,1)S(1)} all-gather(bf16[1,32,2]{1,2,0:T(2,128)(2,1)} %bitcast.268), channel_id=1, replica_groups=mesh['fsdp'=2,'context'=4,'tensor'=4] {'fsdp','context'}, dimensions={0}, use_global_device_ids=true | all-gather | bytes 1152 | tf_op jit(solution)/shard_map/all_gather | solution.py:78
  33.2 27.2 %all-gather.1 = bf16[8,144,4]{1,2,0:T(4,128)(2,1)S(1)} all-gather(bf16[1,144,4]{1,2,0:T(4,128)(2,1)} %bitcast.267), channel_id=1, replica_groups=mesh['fsdp'=2,'context'=4,'tensor'=4] {'fsdp','context'}, dimensions={0}, use_global_device_ids=true | all-gather | bytes 10368 | tf_op jit(solution)/shard_map/all_gather | solution.py:77
  61.1 1.6 fusion.30
  62.8 32.5 %all_gather.32 = bf16[1152,256]{1,0:T(8,128)(2,1)S(1)} all-gather(bf16[144,256]{1,0:T(8,128)(2,1)} %param.20), channel_id=1, replica_groups=mesh['fsdp'=2,'context'=4,'tensor'=4] {'fsdp','context'}, dimensions={0}, use_global_device_ids=true | all-gather | bytes 663552 | tf_op jit(solution)/shard_map/all_gather | solution.py:79
  96.1 2.0 multiply_reduce_fusion.1
  99.1 2.2 fusion.131
  103.1 1.3 collective-permute-start
  104.4 33.8 %all_gather.33 = bf16[1152,256]{1,0:T(8,128)(2,1)S(1)} all-gather(bf16[144,256]{1,0:T(8,128)(2,1)S(1)} %copy-done.31), channel_id=1, replica_groups=mesh['fsdp'=2,'context'=4,'tensor'=4] {'fsdp','context'}, dimensions={0}, use_global_device_ids=true | all-gather | bytes 663552 | tf_op jit(solution)/shard_map/all_gather | solution.py:81
  138.4 2.0 fusion.140
  141.4 1.6 convolution_convert_fusion.5
  143.1 2.3 copy.32
  146.2 35.9 %all-gather.14.cloned.1.call-done = bf16[2048,1152]{1,0:T(8,128)(2,1)} async-done(((bf16[512,1152]{1,0:T(8,128)(2,1)}), bf16[2048,1152]{1,0:T(8,128)(2,1)}) %all-gather.14.cloned.1.call-update) | async-done | bytes 4718608 | tf_op jit(solution)/shard_map/all_gather | solution.py:68
  182.1 3.7 reduce_sum.200
  187.3 2.0 multiply_reduce_fusion
  190.5 117.2 %all-gather.10.cloned.1.call-done = bf16[1152,2,1728]{2,0,1:T(8,128)(2,1)} async-done(((bf16[144,2,1728]{2,0,1:T(8,128)(2,1)}), bf16[1152,2,1728]{2,0,1:T(8,128)(2,1)}) %all-gather.10.cloned.1.call-update) | async-done | bytes 7962640 | tf_op jit(solution)/shard_map/all_gather | solution.py:150
  307.7 8.2 fusion.114
  315.9 2.9 copy-done.7
  318.8 2.4 multiply_convert_fusion
  321.2 58.5 %all-gather.12.cloned.1.call-done = bf16[1152,1728]{1,0:T(8,128)(2,1)} async-done(((bf16[144,1728]{1,0:T(8,128)(2,1)}), bf16[1152,1728]{1,0:T(8,128)(2,1)}) %all-gather.12.cloned.1.call-update) | async-done | bytes 3981328 | tf_op jit(solution)/shard_map/all_gather | solution.py:157
  379.8 6.3 convolution_convert_fusion.4
  386.4 36.0 %all-reduce.12.cloned.1.call-done = bf16[512,1152]{1,0:T(8,128)(2,1)} async-done(((bf16[512,1152]{1,0:T(8,128)(2,1)}), bf16[512,1152]{1,0:T(8,128)(2,1)}) %all-reduce.12.cloned.1.call-update) | async-done | bytes 1179664 | tf_op jit(solution)/shard_map/psum | solution.py:155
  422.4 1.7 fusion.41
  424.1 3.4 fusion.38
  427.6 10.7 multiply_bitcast_fusion
  438.3 1.7 copy-done.81
  440.0 8.1 fusion.7
  448.6 1.3 log_add_fusion
  449.9 36.1 %all-reduce.14.cloned.1.call-done = bf16[512,1152]{1,0:T(8,128)(2,1)} async-done(((bf16[512,1152]{1,0:T(8,128)(2,1)}), bf16[512,1152]{1,0:T(8,128)(2,1)}) %all-reduce.14.cloned.1.call-update) | async-done | bytes 1179664 | tf_op jit(solution)/shard_map/psum | solution.py:179
  486.1 3.6 fusion.29
  489.8 5.1 fusion.25
  501.5 1.4 collective-permute-start.2
  503.9 1.6 convolution_convert_fusion.3
  505.4 11.6 %collective-permute-done.2 = bf16[512,512]{0,1:T(8,128)(2,1)S(1)} collective-permute-done((bf16[512,512]{0,1:T(8,128)(2,1)S(1)}, bf16[512,512]{0,1:T(8,128)(2,1)S(1)}, u32[]{:S(2)}, u32[]{:S(2)}) %collective-permute-start.2) | collective-permute-done | bytes 524320 | tf_op jit(solution)/shard_map/ppermute | solution.py:14
  518.1 1.4 reshape.553
  520.7 1.3 reshape.551
  523.2 7.2 psum.39
  530.4 2.3 fusion.22
  532.8 2.6 fusion.21
  535.3 27.2 %all-reduce.16.cloned.1.call-done = (bf16[512,1152]{1,0:T(8,128)(2,1)}, bf16[512,512]{0,1:T(8,128)(2,1)}) async-done(((bf16[512,1152]{1,0:T(8,128)(2,1)}, bf16[512,512]{0,1:T(8,128)(2,1)}), (bf16[512,1152]{1,0:T(8,128)(2,1)}, bf16[512,512]{0,1:T(8,128)(2,1)})) %all-reduce.16.cloned.1.call-update) | async-done | bytes 1703952 | tf_op jit(solution)/shard_map/psum | solution.py:240
  565.4 3.2 fusion.27
  569.8 1.4 copy.36
  571.3 1.4 pad_maximum_fusion.9
  572.7 1.6 copy.34
  575.9 3.1 convolution_convert_fusion.2
  579.1 9.3 convolution_convert_fusion
  588.4 3.5 slice_bitcast_fusion.1
  591.9 6.4 copy.38
  598.4 6.5 copy.40
  606.5 6.3 convolution_convert_fusion.1
  613.5 4.0 fusion.52
  617.5 16.4 %reduce-scatter.24.cloned.1.call-done = bf16[32,2]{1,0:T(8,128)(2,1)} async-done(((bf16[256,2]{1,0:T(8,128)(2,1)}), bf16[32,2]{1,0:T(8,128)(2,1)}) %reduce-scatter.24.cloned.1.call-update) | async-done | bytes 144
  635.3 60.7 %reduce-scatter.22.cloned.1.call-done = bf16[144,4]{1,0:T(8,128)(2,1)} async-done(((bf16[1152,4]{1,0:T(8,128)(2,1)}), bf16[144,4]{1,0:T(8,128)(2,1)}) %reduce-scatter.22.cloned.1.call-update) | async-done | bytes 1168
  697.5 65.4 %reduce-scatter.16.cloned.1.call-done = bf16[144,2,256]{2,0,1:T(8,128)(2,1)} async-done(((bf16[1152,2,256]{2,0,1:T(8,128)(2,1)}), bf16[144,2,256]{2,0,1:T(8,128)(2,1)}) %reduce-scatter.16.cloned.1.call-update) | async-done | bytes 147472 | tf_op jit(solution)/shard_map/reduce_scatter | solution.py:255
  764.6 65.4 %reduce-scatter.18.cloned.1.call-done = bf16[144,512]{1,0:T(8,128)(2,1)} async-done(((bf16[1152,512]{1,0:T(8,128)(2,1)}), bf16[144,512]{1,0:T(8,128)(2,1)}) %reduce-scatter.18.cloned.1.call-update) | async-done | bytes 147472 | tf_op jit(solution)/shard_map/reduce_scatter | solution.py:273
  829.9 1.7 convert_element_type.219
  831.6 88.8 %reduce-scatter.26.cloned.1.call-done = bf16[144,1728]{1,0:T(8,128)(2,1)} async-done(((bf16[1152,1728]{1,0:T(8,128)(2,1)}), bf16[144,1728]{1,0:T(8,128)(2,1)}) %reduce-scatter.26.cloned.1.call-update) | async-done | bytes 497680
  920.4 2.3 copy.39
  922.6 88.9 %reduce-scatter.28.cloned.1.call-done = bf16[144,1728]{1,0:T(8,128)(2,1)} async-done(((bf16[1152,1728]{1,0:T(8,128)(2,1)}), bf16[144,1728]{1,0:T(8,128)(2,1)}) %reduce-scatter.28.cloned.1.call-update) | async-done | bytes 497680
  1011.5 2.3 copy.41
  1013.8 1.9 maximum_convert_fusion
  1015.7 3.2 copy.33
  1018.8 83.7 %reduce-scatter.20.cloned.1.call-done = bf16[144,1728]{1,0:T(8,128)(2,1)} async-done(((bf16[1152,1728]{1,0:T(8,128)(2,1)}), bf16[144,1728]{1,0:T(8,128)(2,1)}) %reduce-scatter.20.cloned.1.call-update) | async-done | bytes 497680 | tf_op jit(solution)/shard_map/reduce_scatter | solution.py:188
  1102.5 2.1 convert_element_type.223
  (262 shorter events, 35.1 us)
Async XLA Ops:
  7.2 91.9 %all-gather.8.cloned.1.call-start = ((), (), s32[]{:S(2)}) async-start(), calls=%async_computation.7 | async-start | bytes 1327104 | tf_op jit(solution)/shard_map/all_gather | solution.py:80
  7.9 174.2 %all-gather.14.cloned.1.call-start = ((), (), s32[]{:S(2)}) async-start(), calls=%async_computation.15 | async-start | bytes 5898240 | tf_op jit(solution)/shard_map/all_gather | solution.py:68
  8.7 129.6 %collective-permute-start.1 = (s32[2,512]{1,0:T(2,128)S(1)}, s32[2,512]{1,0:T(2,128)S(1)}, u32[]{:S(2)}, u32[]{:S(2)}) collective-permute-start(s32[2,512]{1,0:T(2,128)S(1)} %pad_add_fusion.2), channel_id=1, source_target_pairs={{0,4},{4,8},{8,12},{1,5},{5,9},{9,13},{2,6},{6,10},{10,14},{3,7},{... | collective-permute-start | bytes 12296 | tf_op jit(solution)/shard_map/ppermute | solution.py:14
  14.3 87.4 %copy-start.36 = (f32[512]{0:T(512)}, f32[512]{0:T(512)S(1)}, u32[]{:S(2)}) copy-start(f32[512]{0:T(512)S(1)} %convert_element_type.180) | copy-start | bytes 6148
  60.5 41.2 %copy-start.72 = (f32[128]{0:T(128)}, f32[128]{0:T(128)S(1)}, u32[]{:S(2)}) copy-start(f32[128]{0:T(128)S(1)} %multiply_power_fusion) | copy-start | bytes 1540
  61.1 38.0 %copy-start.43 = (f32[1152]{0:T(1024)}, f32[1152]{0:T(1024)S(1)}, u32[]{:S(2)}) copy-start(f32[1152]{0:T(1024)S(1)} %get-tuple-element.146) | copy-start | bytes 13828
  62.7 36.3 %copy-start.51 = (f32[512]{0:T(512)}, f32[512]{0:T(512)S(1)}, u32[]{:S(2)}) copy-start(f32[512]{0:T(512)S(1)} %fusion.30) | copy-start | bytes 6148
  62.7 36.4 %copy-start.69 = (f32[512]{0:T(512)}, f32[512]{0:T(512)S(1)}, u32[]{:S(2)}) copy-start(f32[512]{0:T(512)S(1)} %fusion.116) | copy-start | bytes 6148
  62.7 36.3 %copy-start.62 = (f32[1,256]{1,0:T(1,128)}, f32[1,256]{1,0:T(1,128)S(1)}, u32[]{:S(2)}) copy-start(f32[1,256]{1,0:T(1,128)S(1)} %get-tuple-element.171) | copy-start | bytes 3076
  62.8 38.8 %copy-start.60 = (f32[1,256]{1,0:T(1,128)}, f32[1,256]{1,0:T(1,128)S(1)}, u32[]{:S(2)}) copy-start(f32[1,256]{1,0:T(1,128)S(1)} %get-tuple-element.172) | copy-start | bytes 3076
  62.8 36.3 %copy-start = (bf16[1,512,1152]{2,1,0:T(8,128)(2,1)S(1)}, bf16[1,512,1152]{2,1,0:T(8,128)(2,1)}, u32[]{:S(2)}) copy-start(bf16[1,512,1152]{2,1,0:T(8,128)(2,1)} %param.15) | copy-start | bytes 3538948
  98.1 3.3 copy-start.41
  101.6 36.7 %copy-start.59 = (s32[1,512]{1,0:T(1,128)S(1)}, s32[1,512]{1,0:T(1,128)}, u32[]{:S(2)}) copy-start(s32[1,512]{1,0:T(1,128)} %param.16) | copy-start | bytes 6148
  101.6 36.7 %copy-start.66 = (s32[1,512]{1,0:T(1,128)S(1)}, s32[1,512]{1,0:T(1,128)}, u32[]{:S(2)}) copy-start(s32[1,512]{1,0:T(1,128)} %param.17) | copy-start | bytes 6148
  103.1 35.3 %collective-permute-start = (bf16[512,512]{0,1:T(8,128)(2,1)S(1)}, bf16[512,512]{0,1:T(8,128)(2,1)S(1)}, u32[]{:S(2)}, u32[]{:S(2)}) collective-permute-start(bf16[512,512]{0,1:T(8,128)(2,1)S(1)} %pad_maximum_fusion.2), channel_id=1, source_target_pairs={{0,4},{4,8},{8,12},{1,5},{5,9},{9,13},{2,6},{6,10},{10,14},{3,7},{... | collective-permute-start | bytes 1572872 | tf_op jit(solution)/shard_map/ppermute | solution.py:14
  138.2 3.1 copy-start.19
  141.4 3.9 copy-start.25
  143.0 164.7 %all-gather.10.cloned.1.call-start = ((), (), s32[]{:S(2)}) async-start(), calls=%async_computation.8 | async-start | bytes 9289728 | tf_op jit(solution)/shard_map/all_gather | solution.py:150
  145.4 234.4 %all-gather.12.cloned.1.call-start = ((), (), s32[]{:S(2)}) async-start(), calls=%async_computation.9 | async-start | bytes 4644864 | tf_op jit(solution)/shard_map/all_gather | solution.py:157
  146.0 276.4 %all-reduce.12.cloned.1.call-start = ((), (), s32[]{:S(2)}) async-start(), calls=%async_computation.10 | async-start | bytes 2359296 | tf_op jit(solution)/shard_map/psum | solution.py:155
  315.9 2.9 copy-start.7
  386.1 100.0 %all-reduce.14.cloned.1.call-start = ((), (), s32[]{:S(2)}) async-start(), calls=%async_computation.11 | async-start | bytes 2359296 | tf_op jit(solution)/shard_map/psum | solution.py:179
  422.4 5.2 copy-start.4
  422.4 5.2 copy-start.11
  424.1 14.2 %copy-start.46 = (f32[512]{0:T(512)}, f32[512]{0:T(512)S(1)}, u32[]{:S(2)}) copy-start(f32[512]{0:T(512)S(1)} %fusion.121) | copy-start | bytes 6148
  424.1 15.9 %slice-start = ((s8[8257536]{0:T(1024)(128)(4,1)}), s8[4194304]{0:T(1024)(128)(4,1)S(1)}, s32[]{:S(2)}) async-start(s8[8257536]{0:T(1024)(128)(4,1)} %bitcast.269), calls=%async_computation.21 | async-start | bytes 8388608
  427.6 10.8 copy-start.76
  427.6 12.5 %slice-start.1 = ((s8[8257536]{0:T(1024)(128)(4,1)}), s8[4063232]{0:T(1024)(128)(4,1)S(1)}, s32[]{:S(2)}) async-start(s8[8257536]{0:T(1024)(128)(4,1)} %bitcast.269), calls=%async_computation.22 | async-start | bytes 8126464
  448.2 114.3 %all-reduce.16.cloned.1.call-start = ((), (), s32[]{:S(2)}) async-start(), calls=%async_computation.20 | async-start | bytes 3407872 | tf_op jit(solution)/shard_map/psum | solution.py:240
  486.1 3.7 copy-start.58
  486.1 3.7 copy-start.1
  486.1 3.7 copy-start.5
  486.1 3.7 copy-start.10
  486.1 3.7 copy-start.29
  486.1 3.7 copy-start.33
  486.1 3.7 copy-start.47
  486.1 3.7 copy-start.49
  489.8 5.1 copy-start.56
  500.2 3.4 copy-start.65
  501.5 15.5 %collective-permute-start.2 = (bf16[512,512]{0,1:T(8,128)(2,1)S(1)}, bf16[512,512]{0,1:T(8,128)(2,1)S(1)}, u32[]{:S(2)}, u32[]{:S(2)}) collective-permute-start(bf16[512,512]{0,1:T(8,128)(2,1)S(1)} %fusion.66), channel_id=1, source_target_pairs={{4,0},{8,4},{12,8},{5,1},{9,5},{13,9},{6,2},{10,6},{14,10},{7,3},{... | collective-permute-start | bytes 1572872 | tf_op jit(solution)/shard_map/ppermute | solution.py:14
  503.9 13.2 %copy-start.24 = (bf16[512,256]{0,1:T(8,128)(2,1)}, bf16[512,256]{0,1:T(8,128)(2,1)S(1)}, u32[]{:S(2)}) copy-start(bf16[512,256]{0,1:T(8,128)(2,1)S(1)} %fusion.108) | copy-start | bytes 786436
  505.4 25.0 %copy-start.16 = (bf16[512,1152]{1,0:T(8,128)(2,1)S(1)}, bf16[512,1152]{1,0:T(8,128)(2,1)}, u32[]{:S(2)}) copy-start(bf16[512,1152]{1,0:T(8,128)(2,1)} %copy-done.15) | copy-start | bytes 3538948
  518.0 14.7 %copy-start.2 = (bf16[1,512,1152]{2,1,0:T(8,128)(2,1)S(1)}, bf16[1,512,1152]{2,1,0:T(8,128)(2,1)}, u32[]{:S(2)}) copy-start(bf16[1,512,1152]{2,1,0:T(8,128)(2,1)} %param.15) | copy-start | bytes 3538948
  518.0 115.9 %reduce-scatter.24.cloned.1.call-start = ((), (), s32[]{:S(2)}) async-start(), calls=%async_computation.17 | async-start | bytes 73728
  532.7 31.0 %copy-start.38 = (f32[512]{0:T(512)S(1)}, f32[512]{0:T(512)}, u32[]{:S(2)}) copy-start(f32[512]{0:T(512)} %copy-done.36) | copy-start | bytes 6148
  532.7 31.0 %copy-start.74 = (f32[128]{0:T(128)S(1)}, f32[128]{0:T(128)}, u32[]{:S(2)}) copy-start(f32[128]{0:T(128)} %copy-done.72) | copy-start | bytes 1540
  532.7 32.2 %copy-start.9 = (f32[512,512]{0,1:T(8,128)S(1)}, f32[512,512]{0,1:T(8,128)}, u32[]{:S(2)}) copy-start(f32[512,512]{0,1:T(8,128)} %copy-done.8) | copy-start | bytes 3145732
  532.7 32.2 %copy-start.40 = (f32[512]{0:T(512)S(1)}, f32[512]{0:T(512)}, u32[]{:S(2)}) copy-start(f32[512]{0:T(512)} %copy-done.39) | copy-start | bytes 6148
  532.7 32.2 %copy-start.61 = (f32[1,256]{1,0:T(1,128)S(1)}, f32[1,256]{1,0:T(1,128)}, u32[]{:S(2)}) copy-start(f32[1,256]{1,0:T(1,128)} %copy-done.60) | copy-start | bytes 3076
  535.3 29.8 %copy-start.54 = (f32[512]{0:T(512)S(1)}, f32[512]{0:T(512)}, u32[]{:S(2)}) copy-start(f32[512]{0:T(512)} %copy-done.53) | copy-start | bytes 6148
  563.7 4.9 copy-start.27
  565.3 3.3 copy-start.28
  565.4 3.9 copy-start.75
  565.4 9.0 copy-start.21
  565.4 9.0 copy-start.26
  571.3 124.7 %reduce-scatter.22.cloned.1.call-start = ((), (), s32[]{:S(2)}) async-start(), calls=%async_computation.16 | async-start | bytes 331776
  574.3 188.6 %reduce-scatter.16.cloned.1.call-start = ((), (), s32[]{:S(2)}) async-start(), calls=%async_computation.12 | async-start | bytes 1327104 | tf_op jit(solution)/shard_map/reduce_scatter | solution.py:255
  575.6 3.4 copy-start.30
  575.6 3.4 copy-start.34
  575.6 3.4 copy-start.50
  575.6 254.3 %reduce-scatter.18.cloned.1.call-start = ((), (), s32[]{:S(2)}) async-start(), calls=%async_computation.13 | async-start | bytes 1327104 | tf_op jit(solution)/shard_map/reduce_scatter | solution.py:273
  579.0 341.4 %reduce-scatter.26.cloned.1.call-start = ((), (), s32[]{:S(2)}) async-start(), calls=%async_computation.18 | async-start | bytes 4644864
  598.3 413.2 %reduce-scatter.28.cloned.1.call-start = ((), (), s32[]{:S(2)}) async-start(), calls=%async_computation.19 | async-start | bytes 4644864
  604.9 497.6 %reduce-scatter.20.cloned.1.call-start = ((), (), s32[]{:S(2)}) async-start(), calls=%async_computation.14 | async-start | bytes 4644864 | tf_op jit(solution)/shard_map/reduce_scatter | solution.py:188
  (37 other events, 58.8 us)
Sparse Core Ops, SparseCore 0:
  10.1 43.7 all-gather.7
  143.1 38.9 all-gather.13
  184.9 122.8 all-gather.9
  309.7 70.0 all-gather.11
  386.2 36.1 all-reduce.11
  448.3 37.7 all-reduce.13
  518.2 44.2 all-reduce.15
  571.4 62.4 reduce-scatter.23
  637.8 58.1 reduce-scatter.21
  699.3 63.6 reduce-scatter.15
  766.3 63.5 reduce-scatter.17
  833.4 86.9 reduce-scatter.25
  923.9 87.5 reduce-scatter.27
  1014.9 87.5 reduce-scatter.19
